TPU v7x, 64 devices: a 2x2x8 block of a 4x4x8 slice. The times are simulated.
64 devices in a mesh: dp: 4 (over x, y), tp: 16 (over z, core).
Axes of the slice: x: 2, y: 2, z: 8, core: 2. Of those that a mesh axis runs over, the one named last changes fastest.
The devices are a block of a 4x4x8 slice.
Arguments:
- hidden: bfloat16 [32, 32, 4096], P('dp'), parts along dimension 0
- tree_mask: int32 [32, 32, 32], P('dp'), parts along dimension 0
- depth: int32 [32, 32], P('dp'), parts along dimension 0
- ctx_len: int32 [32], P('dp'), parts along dimension 0
- block_table: int32 [32, 16], P('dp'), parts along dimension 0
- score_id: int32 [32, 32], P('dp'), parts along dimension 0
- k_cache: bfloat16 [512, 16, 32, 128], P('dp', None, 'tp'), parts along dimension 0
- v_cache: bfloat16 [512, 16, 32, 128], P('dp', None, 'tp'), parts along dimension 0
- attn_norm: bfloat16 [4096], replicated
- w_q: bfloat16 [4096, 4096], P(None, 'tp')
- w_k: bfloat16 [4096, 4096], P(None, 'tp')
- w_v: bfloat16 [4096, 4096], P(None, 'tp')
- w_o: bfloat16 [4096, 4096], P('tp')
- mlp_norm: bfloat16 [4096], replicated
- w_gate: bfloat16 [4096, 11008], P(None, 'tp')
- w_up: bfloat16 [4096, 11008], P(None, 'tp')
- w_down: bfloat16 [11008, 4096], P('tp')
- final_norm: bfloat16 [4096], replicated
- w_lm: bfloat16 [4096, 102400], P(None, 'tp')
Outputs:
- output 1: float32 [32, 32], P('dp'), parts along dimension 0
- output 2: float32 [32, 32], P('dp'), parts along dimension 0
- output 3: bfloat16 [512, 16, 32, 128], P('dp', None, 'tp'), parts along dimension 0
- output 4: bfloat16 [512, 16, 32, 128], P('dp', None, 'tp'), parts along dimension 0
There are 4 independent parts. A program takes and returns all parts, laid end to end along the dimension named above; an argument that names none is the same for every part.
All inputs are finite; a program needn't handle non-finite values.
Results may differ from a plain program's by a relative error of at most 0.0040011.
Values are sent between devices in bfloat16 or wider.
A program may use at most 768 MiB of HBM per device.

v0:
```python
import jax
import jax.numpy as jnp
from jax import lax
from jax.sharding import PartitionSpec as P

RMS_EPS = 1e-5
ROPE_THETA = 500000


def rms_norm(values, gain):
    widened = values.astype(jnp.float32)
    scale = lax.rsqrt(jnp.mean(widened * widened, axis=-1, keepdims=True) + RMS_EPS)
    return (widened * scale * gain.astype(jnp.float32)).astype(jnp.bfloat16)


def rotate(values, positions):
    head_dim = values.shape[-1]
    half = head_dim // 2
    inv_freq = 1.0 / (ROPE_THETA ** (jnp.arange(half, dtype=jnp.float32) * (2.0 / head_dim)))
    angles = positions.astype(jnp.float32)[..., None] * inv_freq
    cosine = jnp.cos(angles)[..., None, :]
    sine = jnp.sin(angles)[..., None, :]
    first = values[..., :half]
    second = values[..., half:]
    return jnp.concatenate([first * cosine - second * sine, second * cosine + first * sine], axis=-1)


def tree_attention(query, key_new, val_new, key_old, val_old, tree_mask, ctx_len):
    scale = query.shape[-1] ** -0.5
    span = key_old.shape[1]
    score_old = jnp.einsum("btkgh,bskh->btkgs", query, key_old, preferred_element_type=jnp.float32) * scale
    seen_old = jnp.arange(span)[None, :] < ctx_len[:, None]
    score_old = jnp.where(seen_old[:, None, None, None, :], score_old, -jnp.inf)
    score_new = jnp.einsum("btkgh,bjkh->btkgj", query, key_new, preferred_element_type=jnp.float32) * scale
    score_new = jnp.where((tree_mask > 0)[:, :, None, None, :], score_new, -jnp.inf)
    top = jnp.maximum(jnp.max(score_old, axis=-1), jnp.max(score_new, axis=-1))[..., None]
    prob_old = jnp.exp(score_old - top)
    prob_new = jnp.exp(score_new - top)
    total = jnp.sum(prob_old, axis=-1) + jnp.sum(prob_new, axis=-1)
    mixed = jnp.einsum("btkgs,bskh->btkgh", prob_old.astype(jnp.bfloat16), val_old, preferred_element_type=jnp.float32)
    mixed = mixed + jnp.einsum("btkgj,bjkh->btkgh", prob_new.astype(jnp.bfloat16), val_new, preferred_element_type=jnp.float32)
    return (mixed / total[..., None]).astype(jnp.bfloat16)


def write_cache(cache, table, ctx_len, new_rows):
    page_size = cache.shape[1]
    slots = ctx_len[:, None] + jnp.arange(new_rows.shape[1])[None, :]
    slot_blocks = jnp.take_along_axis(table, slots // page_size, axis=1)
    return cache.at[slot_blocks, slots % page_size].set(new_rows)


def layer_and_logits(hidden, tree_mask, depth, ctx_len, block_table, k_cache, v_cache, attn_norm, w_q, w_k, w_v, w_o, mlp_norm, w_gate, w_up, w_down, final_norm, w_lm):
    requests = hidden.shape[0]
    nodes = hidden.shape[1]
    page_size = k_cache.shape[1]
    kv_local = k_cache.shape[2]
    head_dim = k_cache.shape[3]
    span = block_table.shape[1] * page_size
    heads_local = w_q.shape[1] // head_dim
    normed = rms_norm(hidden, attn_norm)
    positions = ctx_len[:, None] + depth
    query = jnp.dot(normed, w_q, preferred_element_type=jnp.float32).reshape(requests, nodes, heads_local, head_dim)
    query = rotate(query, positions).astype(jnp.bfloat16).reshape(requests, nodes, kv_local, heads_local // kv_local, head_dim)
    key_new = jnp.dot(normed, w_k, preferred_element_type=jnp.float32).reshape(requests, nodes, kv_local, head_dim)
    key_new = rotate(key_new, positions).astype(jnp.bfloat16)
    val_new = jnp.dot(normed, w_v, preferred_element_type=jnp.float32).astype(jnp.bfloat16).reshape(requests, nodes, kv_local, head_dim)
    key_old = k_cache[block_table].reshape(requests, span, kv_local, head_dim)
    val_old = v_cache[block_table].reshape(requests, span, kv_local, head_dim)
    attended = tree_attention(query, key_new, val_new, key_old, val_old, tree_mask, ctx_len).reshape(requests, nodes, heads_local * head_dim)
    attn_sum = lax.psum(jnp.dot(attended, w_o, preferred_element_type=jnp.float32).astype(jnp.bfloat16), "tp")
    residual = (hidden.astype(jnp.float32) + attn_sum.astype(jnp.float32)).astype(jnp.bfloat16)
    normed_mlp = rms_norm(residual, mlp_norm)
    gate = jnp.dot(normed_mlp, w_gate, preferred_element_type=jnp.float32)
    upper = jnp.dot(normed_mlp, w_up, preferred_element_type=jnp.float32)
    product = (jax.nn.silu(gate) * upper).astype(jnp.bfloat16)
    mlp_sum = lax.psum(jnp.dot(product, w_down, preferred_element_type=jnp.float32).astype(jnp.bfloat16), "tp")
    layer_out = (residual.astype(jnp.float32) + mlp_sum.astype(jnp.float32)).astype(jnp.bfloat16)
    logits = jnp.dot(rms_norm(layer_out, final_norm), w_lm, preferred_element_type=jnp.float32)
    return logits, key_new, val_new


def solution(mesh):
    def group_step(hidden, tree_mask, depth, ctx_len, block_table, score_id, k_cache, v_cache, attn_norm, w_q, w_k, w_v, w_o, mlp_norm, w_gate, w_up, w_down, final_norm, w_lm):
        logits, key_new, val_new = layer_and_logits(hidden, tree_mask, depth, ctx_len, block_table, k_cache, v_cache, attn_norm, w_q, w_k, w_v, w_o, mlp_norm, w_gate, w_up, w_down, final_norm, w_lm)
        vocab_local = logits.shape[-1]
        global_top = lax.pmax(jnp.max(logits, axis=-1), "tp")
        part_sum = jnp.sum(jnp.exp(logits - global_top[..., None]), axis=-1)
        local_id = score_id - lax.axis_index("tp") * vocab_local
        inside = (local_id >= 0) & (local_id < vocab_local)
        picked = jnp.take_along_axis(logits, jnp.clip(local_id, 0, vocab_local - 1)[..., None], axis=-1)[..., 0]
        summed = lax.psum(jnp.stack([part_sum, jnp.where(inside, picked, 0.0)]), "tp")
        log_norm = global_top + jnp.log(summed[0])
        log_prob = summed[1] - log_norm
        return log_norm, log_prob, write_cache(k_cache, block_table, ctx_len, key_new), write_cache(v_cache, block_table, ctx_len, val_new)

    request_spec = P("dp", None, None)
    node_spec = P("dp", None)
    cache_spec = P("dp", None, "tp", None)
    shared_spec = P(None)
    column_spec = P(None, "tp")
    row_spec = P("tp", None)
    in_specs = (request_spec, request_spec, node_spec, P("dp"), node_spec, node_spec, cache_spec, cache_spec, shared_spec, column_spec, column_spec, column_spec, row_spec, shared_spec, column_spec, column_spec, row_spec, shared_spec, column_spec)
    out_specs = (node_spec, node_spec, cache_spec, cache_spec)
    return jax.shard_map(group_step, mesh=mesh, in_specs=in_specs, out_specs=out_specs, check_vma=False)
```

profile of v0, /device:TPU:21, one launch (start us, length us, event | category | flops | bytes accessed | tf_op | source)
XLA Modules:
  0.0 374.0 jit_solution(11534447085836806295)
XLA Ops:
  7.3 1.4 copy.72
  8.7 2.9 copy.73
  11.9 2.1 fusion.14
  14.1 3.8 %fusion.49 = bf16[8,32,256]{2,1,0:T(8,128)(2,1)} fusion(bf16[4096,256]{1,0:T(8,128)(2,1)} %param.32, bf16[8,32,4096]{2,1,0:T(8,128)(2,1)} %param.21, f32[4096]{0:T(1024)S(1)} %convert_element_type.72, f32[8,32]{1,0:T(8,128)S(1)} %add_rsqrt_fusion.2), kind=kOutput, calls=%fused_computation.55 | convolution fusion | flops 541130752 | bytes 4342784 | tf_op jit(solution)/shard_map/dot_general | solution.py:66
  17.9 1.5 fusion.26
  19.4 1.1 reshape.249
  20.5 3.7 fusion.28
  24.2 1.8 reshape.248
  26.0 4.8 %gather_fusion = bf16[128,16,2,128]{3,2,1,0:T(2,128)(2,1)} fusion(bf16[128,16,2,128]{3,2,1,0:T(2,128)(2,1)} %copy.73, s32[1024]{0:T(1024)S(1)} %pad_clamp_fusion), kind=kCustom, calls=%fused_computation.1 | custom fusion | bytes 2097664 | tf_op jit(solution)/shard_map/gather | solution.py:68
  30.8 3.6 gather_fusion.1
  34.4 0.5 multiply_cosine_fusion
  34.9 1.8 fusion.98
  37.0 0.3 fusion.101
  37.3 0.6 fusion.100
  38.2 0.3 fusion.58
  39.1 2.0 convolution_convert_fusion
  41.4 113.1 %all-reduce.3.cloned.1.call-done = bf16[8,32,4096]{2,1,0:T(8,128)(2,1)} async-done(((bf16[8,32,4096]{2,1,0:T(8,128)(2,1)}), bf16[8,32,4096]{2,1,0:T(8,128)(2,1)}) %all-reduce.3.cloned.1.call-update) | async-done | bytes 2097168 | tf_op jit(solution)/shard_map/psum | solution.py:70
  154.6 3.3 fusion.18
  157.9 5.6 %fusion.6 = f32[8,32,688]{2,1,0:T(8,128)S(1)} fusion(bf16[4096,688]{0,1:T(8,128)(2,1)} %param.35, bf16[8,32,4096]{2,1,0:T(8,128)(2,1)S(1)} %get-tuple-element.8, f32[4096]{0:T(1024)S(1)} %convert_element_type.83, f32[8,32]{1,0:T(8,128)S(1)} %add_rsqrt_fusion.1), kind=kOutput, calls=%fused_computation.19 | convolution fusion | flops 1447034880 | bytes 8455168 | tf_op jit(solution)/shard_map/dot_general | solution.py:73
  163.6 2.2 fusion.39
  165.8 3.1 fusion.8
  169.2 1.4 gather_fusion.3
  171.2 29.8 %scatter_fusion.1 = bf16[128,16,2,128]{3,2,1,0:T(2,128)(2,1)} fusion(bf16[128,16,2,128]{3,2,1,0:T(2,128)(2,1)} %copy.73, s32[256]{0:T(256)S(1)} %reshape.285, bf16[256,2,128]{2,1,0:T(2,128)(2,1)S(1)} %reshape.293), kind=kCustom, calls=%fused_computation.5 | custom fusion | bytes 395264 | tf_op jit(solution)/shard_map/scatter | solution.py:49
  200.9 10.1 %scatter_fusion = bf16[128,16,2,128]{3,2,1,0:T(2,128)(2,1)S(1)} fusion(bf16[128,16,2,128]{3,2,1,0:T(2,128)(2,1)S(1)} %copy.72, s32[256]{0:T(256)S(1)} %reshape.285, bf16[256,2,128]{2,1,0:T(2,128)(2,1)S(1)} %copy.41), kind=kCustom, calls=%fused_computation.4 | custom fusion | bytes 395264 | tf_op jit(solution)/shard_map/scatter | solution.py:49
  211.1 67.3 %all-reduce.5.cloned.1.call-done = bf16[8,32,4096]{2,1,0:T(8,128)(2,1)} async-done(((bf16[8,32,4096]{2,1,0:T(8,128)(2,1)}), bf16[8,32,4096]{2,1,0:T(8,128)(2,1)}) %all-reduce.5.cloned.1.call-update) | async-done | bytes 2097168 | tf_op jit(solution)/shard_map/psum | solution.py:76
  278.3 3.1 fusion.11
  281.5 25.8 %fusion.102 = (f32[8,32]{1,0:T(8,128)S(1)}, f32[8,32,6400]{2,1,0:T(8,128)}) fusion(bf16[4096,6400]{1,0:T(8,128)(2,1)} %param.39, f32[4096]{0:T(1024)S(1)} %convert_element_type.90, f32[8,32]{1,0:T(8,128)S(1)} %add_rsqrt_fusion, bf16[8,32,4096]{2,1,0:T(8,128)(2,1)S(1)} %copy-done.7, bf16[8,32,4096]{2,1,0:T(8,128)(2,1)} %copy-done.3), kind=kOutput, calls=%fused_computation.143 | convolution fusion | flops 13431799808 | bytes 63195136 | tf_op jit(solution)/shard_map/dot_general | solution.py:78
  307.3 23.9 %pmax.7 = f32[8,32]{1,0:T(8,128)S(1)} all-reduce(f32[8,32]{1,0:T(8,128)S(1)} %get-tuple-element.25), channel_id=1, replica_groups=mesh['dp'=4,'tp'=16] {'tp'}, use_global_device_ids=true, to_apply=%region_10.11 | all-reduce | flops 256 | bytes 2048 | tf_op jit(solution)/shard_map/pmax | solution.py:86
  331.2 4.5 %gather_fusion.2 = f32[256]{0:T(256)S(1)} fusion(f32[8,32,6400]{2,1,0:T(8,128)} %get-tuple-element.26, s32[256]{0:T(256)S(1)} %reshape.279), kind=kCustom, calls=%fused_computation.3 | custom fusion | bytes 5120 | tf_op jit(solution)/shard_map/jit(take_along_axis)/gather | solution.py:90
  335.7 3.9 %exponential_reduce_fusion = f32[8,32]{1,0:T(8,128)S(1)} fusion(f32[8,32,6400]{2,1,0:T(8,128)} %get-tuple-element.26, f32[8,32]{1,0:T(8,128)S(1)} %pmax.7), kind=kLoop, calls=%fused_computation.8 | loop fusion | flops 3276544 | bytes 6555648 | tf_op jit(solution)/shard_map/reduce_sum | solution.py:87
  339.7 26.9 %psum.23 = f32[2,8,32]{2,1,0:T(8,128)S(1)} all-reduce(f32[2,8,32]{2,1,0:T(8,128)S(1)} %pad_maximum_fusion.4), channel_id=1, replica_groups=mesh['dp'=4,'tp'=16] {'tp'}, use_global_device_ids=true, to_apply=%region_12.13 | all-reduce | flops 512 | bytes 4096 | tf_op jit(solution)/shard_map/psum | solution.py:91
  366.5 0.6 fusion.79
  (92 shorter events, 2.8 us)
Async XLA Ops:
  7.2 31.9 %copy-start = (bf16[256,4096]{1,0:T(8,128)(2,1)S(1)}, bf16[256,4096]{1,0:T(8,128)(2,1)}, u32[]{:S(2)}) copy-start(bf16[256,4096]{1,0:T(8,128)(2,1)} %param.33) | copy-start | bytes 6291460
  7.2 6.8 %copy-start.9 = (s32[8,32,32]{2,1,0:T(8,128)S(1)}, s32[8,32,32]{2,1,0:T(8,128)}, u32[]{:S(2)}) copy-start(s32[8,32,32]{2,1,0:T(8,128)} %param.22) | copy-start | bytes 98308
  7.2 4.5 %copy-start.17 = (s32[8,32]{1,0:T(8,128)S(1)}, s32[8,32]{1,0:T(8,128)}, u32[]{:S(2)}) copy-start(s32[8,32]{1,0:T(8,128)} %param.23) | copy-start | bytes 3076
  7.2 4.4 %copy-start.13 = (s32[8]{0:T(128)S(1)}, s32[8]{0:T(128)}, u32[]{:S(2)}) copy-start(s32[8]{0:T(128)} %param.24) | copy-start | bytes 100
  7.2 4.5 %copy-start.2 = (s32[8,16]{1,0:T(8,128)S(1)}, s32[8,16]{1,0:T(8,128)}, u32[]{:S(2)}) copy-start(s32[8,16]{1,0:T(8,128)} %param.25) | copy-start | bytes 1540
  7.2 6.7 %copy-start.14 = (bf16[4096]{0:T(1024)(128)(2,1)S(1)}, bf16[4096]{0:T(1024)(128)(2,1)}, u32[]{:S(2)}) copy-start(bf16[4096]{0:T(1024)(128)(2,1)} %param.29) | copy-start | bytes 24580
  7.2 147.3 %all-reduce.3.cloned.1.call-start = ((), (), s32[]{:S(2)}) async-start(), calls=%async_computation | async-start | bytes 4194304 | tf_op jit(solution)/shard_map/psum | solution.py:70
  14.1 3.8 %copy-start.4 = (bf16[8,32,4096]{2,1,0:T(8,128)(2,1)S(1)}, bf16[8,32,4096]{2,1,0:T(8,128)(2,1)}, u32[]{:S(2)}) copy-start(bf16[8,32,4096]{2,1,0:T(8,128)(2,1)} %param.21) | copy-start | bytes 6291460
  14.1 3.8 %copy-start.18 = (bf16[4096,256]{1,0:T(8,128)(2,1)S(1)}, bf16[4096,256]{1,0:T(8,128)(2,1)}, u32[]{:S(2)}) copy-start(bf16[4096,256]{1,0:T(8,128)(2,1)} %param.31) | copy-start | bytes 6291460
  34.4 2.9 copy-start.8
  34.4 3.8 %copy-start.6 = (bf16[128,16,2,128]{3,2,1,0:T(2,128)(2,1)S(1)}, bf16[128,16,2,128]{3,2,1,0:T(2,128)(2,1)}, u32[]{:S(2)}) copy-start(bf16[128,16,2,128]{3,2,1,0:T(2,128)(2,1)} %gather_fusion) | copy-start | bytes 3145732
  36.7 1.9 copy-start.10
  38.6 2.8 copy-start.15
  41.2 237.2 %all-reduce.5.cloned.1.call-start = ((), (), s32[]{:S(2)}) async-start(), calls=%async_computation.1 | async-start | bytes 4194304 | tf_op jit(solution)/shard_map/psum | solution.py:76
  154.6 9.0 %slice-start = ((s8[5636096]{0:T(1024)(128)(4,1)}), s8[4194304]{0:T(1024)(128)(4,1)S(1)}, s32[]{:S(2)}) async-start(s8[5636096]{0:T(1024)(128)(4,1)} %bitcast.111), calls=%async_computation.2 | async-start | bytes 8388608
  154.6 11.2 %slice-start.2 = ((s8[5636096]{0:T(1024)(128)(4,1)}), s8[4194304]{0:T(1024)(128)(4,1)S(1)}, s32[]{:S(2)}) async-start(s8[5636096]{0:T(1024)(128)(4,1)} %bitcast.113), calls=%async_computation.4 | async-start | bytes 8388608
  157.9 5.7 %copy-start.3 = (bf16[8,32,4096]{2,1,0:T(8,128)(2,1)}, bf16[8,32,4096]{2,1,0:T(8,128)(2,1)S(1)}, u32[]{:S(2)}) copy-start(bf16[8,32,4096]{2,1,0:T(8,128)(2,1)S(1)} %get-tuple-element.8) | copy-start | bytes 6291460
  157.9 5.7 %slice-start.1 = ((s8[5636096]{0:T(1024)(128)(4,1)}), s8[1441792]{0:T(1024)(128)(4,1)S(1)}, s32[]{:S(2)}) async-start(s8[5636096]{0:T(1024)(128)(4,1)} %bitcast.111), calls=%async_computation.3 | async-start | bytes 2883584
  157.9 7.9 %slice-start.3 = ((s8[5636096]{0:T(1024)(128)(4,1)}), s8[1441792]{0:T(1024)(128)(4,1)S(1)}, s32[]{:S(2)}) async-start(s8[5636096]{0:T(1024)(128)(4,1)} %bitcast.113), calls=%async_computation.5 | async-start | bytes 2883584
  165.8 3.2 copy-start.11
  168.9 2.0 copy-start.12
  168.9 2.1 copy-start.16
  211.1 96.2 %copy-start.5 = (bf16[128,16,2,128]{3,2,1,0:T(2,128)(2,1)}, bf16[128,16,2,128]{3,2,1,0:T(2,128)(2,1)S(1)}, u32[]{:S(2)}) copy-start(bf16[128,16,2,128]{3,2,1,0:T(2,128)(2,1)S(1)} %scatter_fusion) | copy-start | bytes 3145732
  278.3 3.1 copy-start.7
  331.2 36.0 %copy-start.1 = (bf16[256,4096]{1,0:T(8,128)(2,1)S(1)}, bf16[256,4096]{1,0:T(8,128)(2,1)}, u32[]{:S(2)}) copy-start(bf16[256,4096]{1,0:T(8,128)(2,1)} %param.33) | copy-start | bytes 6291460
Sparse Core Ops, SparseCore 0:
  41.3 113.2 all-reduce.2
  169.1 109.1 all-reduce.4
where the time goes:
time: 375 us; the launch traced here: 374 us
  waiting for transfers between devices  180 us (48%)
  local copies, waits for them, and re-layouts  64.2 us (17%)
  blocking collectives  50.7 us (14%)
  matrix products  49.1 us (13%)
  other arithmetic  14.6 us (4%)
  between operations  14.5 us (4%)
    psum x1, waiting for transfers between devices, layer_and_logits(): lax.psum(jnp.dot(attended, w_o, preferred_element_type=jnp.float32).astyp...  113 us
    psum x1, waiting for transfers between devices, layer_and_logits(): lax.psum(jnp.dot(product, w_down, preferred_element_type=jnp.float32).ast...  67.3 us
    scatter x2, local copies, waits for them, and re-layouts, write_cache(): return cache.at[slot_blocks, slots % page_size].set(new_rows)  39.9 us
    psum x1, blocking collectives, group_step(): lax.psum(jnp.stack([part_sum, jnp.where(inside, picked, 0.0)]), 'tp')  26.9 us
    dot_general x1, matrix products, layer_and_logits(): jnp.dot(rms_norm(layer_out, final_norm), w_lm, preferred_element_type=jnp...  25.8 us
    pmax x1, blocking collectives, group_step(): global_top = lax.pmax(jnp.max(logits, axis=-1), 'tp')  23.9 us
    reduce_sum x3, other arithmetic, rms_norm(): jnp.mean(widened * widened, axis=-1, keepdims=True) + RMS_EPS  8.54 us
  transfers between devices with their start and end apart: 2, of which 2 were waited for; matrix products, arithmetic and copies ran while one was open for 11% of the time, Pallas kernels for 0%

commit v1 on v0

v1 whole, which is shorter than its diff:
```python
import functools

import jax
import jax.numpy as jnp
import numpy as np
from jax import lax
from jax.experimental import pallas as pl
from jax.experimental.pallas import tpu as pltpu
from jax.sharding import PartitionSpec as P

RMS_EPS = 1e-5
ROPE_THETA = 500000
NEG = -1e30
CHUNKS = 4
SLOTS = 3
F32 = jnp.float32
BF16 = jnp.bfloat16


def dot(a, b):
    return lax.dot_general(a, b, (((1,), (0,)), ((), ())), preferred_element_type=F32)


def dot_t(a, b):
    return lax.dot_general(a, b, (((1,), (1,)), ((), ())), preferred_element_type=F32)


def iota(shape, axis):
    return lax.broadcasted_iota(jnp.int32, shape, axis)


def attention_kernel(dims, ctx_ref, table_ref, mask_ref, freq_ref, gain_ref, hid_hbm, wq_hbm, wk_hbm, wv_hbm, kc_hbm, vc_hbm, att_ref, ko_hbm, vo_hbm, hid, wq, wk, wv, kc, vc, normed, sumsq, in_sem, out_sem):
    requests, nodes, pages, page = dims
    rows, width = hid.shape
    head_dim = freq_ref.shape[1]
    heads = wq.shape[1] // head_dim
    pairs = [(hid_hbm, hid), (wq_hbm, wq), (wk_hbm, wk), (kc_hbm, kc), (wv_hbm, wv), (vc_hbm, vc)]
    copies = [pltpu.make_async_copy(src, dst, in_sem.at[i]) for i, (src, dst) in enumerate(pairs)]
    for copy in copies:
        copy.start()

    tree = mask_ref[...]
    depth = jnp.sum(tree, axis=1, keepdims=True) - 1
    position = jnp.concatenate([depth[b * nodes : (b + 1) * nodes] + ctx_ref[b] for b in range(requests)], axis=0)
    angle = position.astype(F32) * freq_ref[...]
    cosine = jnp.cos(angle)
    sine = jnp.sin(angle)
    sine = jnp.where(iota(sine.shape, 1) < head_dim // 2, -sine, sine)

    copies[0].wait()
    step = 32

    def square(i, carry):
        at = pl.ds(pl.multiple_of(i * step, step), step)
        total = jnp.zeros((step, 128), F32)
        for j in range(width // 512):
            x = hid[at, j * 512 : (j + 1) * 512].astype(F32)
            x = x * x
            total = total + ((x[:, :128] + x[:, 128:256]) + (x[:, 256:384] + x[:, 384:]))
        sumsq[at, :] = total
        return carry

    lax.fori_loop(0, rows // step, square, 0)
    scale = lax.rsqrt(jnp.sum(sumsq[...], axis=1, keepdims=True) * (1.0 / width) + RMS_EPS)
    sumsq[...] = jnp.broadcast_to(scale, sumsq.shape)

    def apply(i, carry):
        at = pl.ds(pl.multiple_of(i * step, step), step)
        s = sumsq[at, :]
        s = jnp.concatenate([s] * 4, axis=1)
        for j in range(width // 512):
            cols = slice(j * 512, (j + 1) * 512)
            normed[at, cols] = (hid[at, cols].astype(F32) * s * gain_ref[:, cols]).astype(BF16)
        return carry

    lax.fori_loop(0, rows // step, apply, 0)

    def rotate(x):
        return (x * cosine + pltpu.roll(x, head_dim // 2, 1) * sine).astype(BF16)

    def by_head(x):
        return [x[:, h * head_dim : (h + 1) * head_dim] for h in range(heads)]

    copies[1].wait()
    query = [rotate(x) for x in by_head(dot(normed[...], wq[...]))]
    copies[2].wait()
    key_new = [rotate(x) for x in by_head(dot(normed[...], wk[...]))]
    copies[4].wait()
    val_new = [x.astype(BF16) for x in by_head(dot(normed[...], wv[...]))]

    def stack(parts, b):
        return jnp.concatenate([x[b * nodes : (b + 1) * nodes] for x in parts], axis=0)

    queries = [stack(query, b) for b in range(requests)]
    keys = [stack(key_new, b) for b in range(requests)]
    vals = [stack(val_new, b) for b in range(requests)]

    copies[3].wait()
    copies[5].wait()
    n_pages = nodes // page + 1
    wide = page * heads
    for b in range(requests):
        ctx = ctx_ref[b]
        first = ctx // page
        off = ctx - first * page
        r = iota((n_pages * wide, heads * nodes), 0)
        c = iota((n_pages * wide, heads * nodes), 1)
        j = r // heads - off
        pick = (j >= 0) & (j < nodes) & (c == (r % heads) * nodes + j)
        onehot = jnp.where(pick, 1.0, 0.0).astype(BF16)
        for cache, new in ((kc, keys[b]), (vc, vals[b])):
            window = dot(onehot, new)
            for p in range(n_pages):
                block = table_ref[b, jnp.minimum(first + p, pages - 1)]
                slot = iota((wide, head_dim), 0) // heads + (p * page) - off
                old = cache[block].astype(F32)
                cache[block] = jnp.where((slot >= 0) & (slot < nodes), window[p * wide : (p + 1) * wide], old).astype(BF16)
    outs = [pltpu.make_async_copy(kc, ko_hbm, out_sem.at[0]), pltpu.make_async_copy(vc, vo_hbm, out_sem.at[1])]
    for copy in outs:
        copy.start()

    span = pages * wide
    many = heads * nodes
    factor = head_dim**-0.5
    same_old = iota((many, span), 1) % heads == iota((many, span), 0) // nodes
    slot_old = iota((many, span), 1) // heads
    same_new = iota((many, many), 1) // nodes == iota((many, many), 0) // nodes
    old_scores, new_scores = [], []
    for b in range(requests):
        k_old = jnp.concatenate([kc[table_ref[b, p]] for p in range(pages)], axis=0)
        s_old = dot_t(queries[b], k_old) * factor
        old_scores.append(jnp.where(same_old & (slot_old < ctx_ref[b]), s_old, NEG))
        seen = tree[b * nodes : (b + 1) * nodes]
        seen = jnp.concatenate([seen] * heads, axis=1)
        seen = jnp.concatenate([seen] * heads, axis=0)
        s_new = dot_t(queries[b], keys[b]) * factor
        new_scores.append(jnp.where(same_new & (seen > 0), s_new, NEG))
    for b in range(requests):
        top = jnp.maximum(jnp.max(old_scores[b], axis=1, keepdims=True), jnp.max(new_scores[b], axis=1, keepdims=True))
        p_old = jnp.exp(old_scores[b] - top)
        p_new = jnp.exp(new_scores[b] - top)
        total = jnp.sum(p_old, axis=1, keepdims=True) + jnp.sum(p_new, axis=1, keepdims=True)
        v_old = jnp.concatenate([vc[table_ref[b, p]] for p in range(pages)], axis=0)
        mixed = dot(p_old.astype(BF16), v_old) + dot(p_new.astype(BF16), vals[b])
        mixed = (mixed / total).astype(BF16)
        for h in range(heads):
            att_ref[b * nodes : (b + 1) * nodes, h * head_dim : (h + 1) * head_dim] = mixed[h * nodes : (h + 1) * nodes]
    for copy in outs:
        copy.wait()


def attention(hidden, tree_mask, ctx_len, block_table, k_cache, v_cache, attn_norm, w_q, w_k, w_v):
    requests, nodes, width = hidden.shape
    blocks, page, heads, head_dim = k_cache.shape
    pages = block_table.shape[1]
    rows = requests * nodes
    half = head_dim // 2
    inv_freq = 1.0 / (np.float32(ROPE_THETA) ** (np.arange(half, dtype=np.float32) * np.float32(2.0 / head_dim)))
    freq = jnp.asarray(np.concatenate([inv_freq, inv_freq])[None].astype(np.float32))
    pages_shape = (blocks, page * heads, head_dim)
    vmem = pl.BlockSpec(memory_space=pltpu.VMEM)
    smem = pl.BlockSpec(memory_space=pltpu.SMEM)
    hbm = pl.BlockSpec(memory_space=pl.ANY)
    cache = jax.ShapeDtypeStruct(pages_shape, BF16)
    local = w_q.shape[1]
    att, k_out, v_out = pl.pallas_call(
        functools.partial(attention_kernel, (requests, nodes, pages, page)),
        name="tree_attention",
        out_shape=(jax.ShapeDtypeStruct((rows, local), BF16), cache, cache),
        in_specs=[smem, smem, vmem, vmem, vmem] + [hbm] * 6,
        out_specs=(vmem, hbm, hbm),
        scratch_shapes=[
            pltpu.VMEM((rows, width), BF16),
            pltpu.VMEM((width, local), BF16),
            pltpu.VMEM((width, local), BF16),
            pltpu.VMEM((width, local), BF16),
            pltpu.VMEM(pages_shape, BF16),
            pltpu.VMEM(pages_shape, BF16),
            pltpu.VMEM((rows, width), BF16),
            pltpu.VMEM((rows, 128), F32),
            pltpu.SemaphoreType.DMA((6,)),
            pltpu.SemaphoreType.DMA((2,)),
        ],
        compiler_params=pltpu.CompilerParams(vmem_limit_bytes=67043328),
    )(
        ctx_len,
        block_table,
        tree_mask.reshape(rows, nodes),
        freq,
        attn_norm.astype(F32)[None],
        hidden.reshape(rows, width),
        w_q,
        w_k,
        w_v,
        k_cache.reshape(pages_shape),
        v_cache.reshape(pages_shape),
    )
    return att, k_out.reshape(k_cache.shape), v_out.reshape(v_cache.shape)


def layer_kernel(n, ids_ref, gm_ref, gf_ref, att_hbm, hid_hbm, wo_hbm, wg_hbm, wu_hbm, wd_hbm, wlm_hbm, ln_ref, lp_ref, *scratch):
    (
        att, hid, wo, wg, wu, wd, wlm, acc, gate, up, prod, xn, scale_ref, own, d2d_send, d2d_recv, rs_send, rs_recv, mine, part,
        ssq_send, ssq_recv, st_send, st_recv, lanes,
        load_sem, lm_sem, pair_sems, pair_recv, rs_sems, rs_rsem, ag_sems, ag_rsem, hp_sems, hp_rsem, sq_sems, sq_rsem, st_sems, st_rsem,
    ) = scratch
    chips = n // 2
    far = chips // 2
    rows, cb = hid.shape
    rc = rows // CHUNKS
    half = CHUNKS // 2
    width = cb * n
    me = lax.axis_index("tp")
    z, c = me // 2, me % 2
    partner = z * 2 + (1 - c)
    ring = (lax.rem(z + 1, chips) * 2 + c, lax.rem(z + chips - 1, chips) * 2 + c)

    def remote(src, dst, send, recv, device):
        return pltpu.make_async_remote_copy(
            src_ref=src, dst_ref=dst, send_sem=send, recv_sem=recv, device_id={"tp": device}, device_id_type=pl.DeviceIdType.MESH
        )

    sent = []

    def start(copy):
        copy.start()
        sent.append(copy)

    def drain():
        while sent:
            sent.pop(0).wait_send()

    def chip_at(offset):
        return lax.rem(z + offset, chips)

    loads = [
        pltpu.make_async_copy(src, dst, load_sem.at[i])
        for i, (src, dst) in enumerate(
            [
                (att_hbm, att),
                (wo_hbm, wo),
                (hid_hbm.at[:, pl.ds(pl.multiple_of(me * cb, cb), cb)], hid),
                (wg_hbm, wg),
                (wu_hbm, wu),
                (wd_hbm, wd),
            ]
        )
    ]
    for copy in loads[:3]:
        copy.start()
    barrier = pltpu.get_barrier_semaphore()
    for k in range(1, n):
        pl.semaphore_signal(barrier, inc=1, device_id={"tp": lax.rem(me + k, n)}, device_id_type=pl.DeviceIdType.MESH)
    pl.semaphore_wait(barrier, n - 1)
    for copy in loads[3:]:
        copy.start()

    consume = [0]
    for d in range(1, far):
        consume += [chips - d, d]
    consume += [far]

    def lm_load(j):
        at = pl.multiple_of(chip_at(consume[j]) * (2 * cb), 2 * cb)
        return pltpu.make_async_copy(wlm_hbm.at[pl.ds(at, 2 * cb)], wlm.at[j % SLOTS], lm_sem.at[j % SLOTS])

    for j in range(SLOTS):
        lm_load(j).start()

    order = [far]
    for d in range(far - 1, 0, -1):
        order += [d, chips - d]
    order += [0]

    def reduce_scatter(ph, lhs, weight):
        waited = set()

        def compute(i):
            base = chip_at(order[i]) * (2 * cb)
            other = pl.ds(pl.multiple_of(base + (1 - c) * cb, cb), cb)
            d2d_send[i] = dot(lhs, weight[:, other]).astype(BF16)
            start(remote(d2d_send.at[i], d2d_recv.at[ph, i], pair_sems.at[i], pair_recv.at[ph, i], partner))
            own[i] = dot(lhs, weight[:, pl.ds(pl.multiple_of(base + c * cb, cb), cb)])

        def local(i, k):
            if i not in waited:
                waited.add(i)
                remote(d2d_send.at[i], d2d_recv.at[ph, i], pair_sems.at[i], pair_recv.at[ph, i], partner).wait_recv()
            at = slice(k * rc, (k + 1) * rc)
            return own[i, at, :] + d2d_recv[ph, i, at, :].astype(F32)

        def unit(way, d, k):
            return remote(rs_send.at[way, d - 1, k], rs_recv.at[ph, way, d - 1, k], rs_sems.at[way, d - 1, k], rs_rsem.at[ph, way, d - 1, k], ring[way])

        def far_half(way):
            return range(half) if way == 0 else range(half, CHUNKS)

        def near_half(way):
            return range(half, CHUNKS) if way == 0 else range(half)

        def hop(d):
            for part_of in (near_half, far_half):
                if d == far and part_of is near_half:
                    continue
                for q in range(half):
                    for way in (0, 1):
                        k = part_of(way)[q]
                        i = order.index(d if way == 0 else chips - d)
                        value = local(i, k)
                        if d + 1 < far or (d + 1 == far and k in far_half(way)):
                            unit(way, d + 1, k).wait_recv()
                            value = value + rs_recv[ph, way, d, k].astype(F32)
                        rs_send[way, d - 1, k] = value.astype(BF16)
                        start(unit(way, d, k))

        compute(0)
        done = 1
        for d in range(far, 0, -1):
            ahead = 2 if d > 1 else 1
            for _ in range(ahead):
                if done < chips:
                    compute(done)
                    done += 1
            hop(d)
        while done < chips:
            compute(done)
            done += 1
        sums = []
        last = order.index(0)
        for k in range(CHUNKS):
            value = local(last, k)
            for way in (0, 1):
                unit(way, 1, k).wait_recv()
                value = value + rs_recv[ph, way, 0, k].astype(F32)
            sums.append(value.astype(BF16))
        return sums

    def broadcast_sumsq(ph, squares):
        ssq_send[...] = jnp.sum(jnp.transpose(squares), axis=0, keepdims=True)
        ssq_recv[ph, me] = ssq_send[...]
        for k in range(1, n):
            start(remote(ssq_send, ssq_recv.at[ph, me], sq_sems.at[k], sq_rsem.at[ph, me], lax.rem(me + k, n)))

    def wait_scale(ph):
        for k in range(1, n):
            src = lax.rem(me + k, n)
            remote(ssq_send, ssq_recv.at[ph, src], sq_sems.at[k], sq_rsem.at[ph, src], src).wait_recv()
        total = ssq_recv[ph, 0]
        for j in range(1, n):
            total = total + ssq_recv[ph, j]
        scale = lax.rsqrt(total * (1.0 / width) + RMS_EPS)
        scale_ref[...] = jnp.transpose(jnp.broadcast_to(scale, (128, rows)))

    def residual_gather(ph, sums, before, gain_ref, block):
        squares = jnp.zeros((rows, 128), F32)
        wides = []
        for k in range(CHUNKS):
            at = slice(k * rc, (k + 1) * rc)
            value = (before[at, :].astype(F32) + sums[k].astype(F32)).astype(BF16)
            mine[ph, 0, at, :] = value
            value = value.astype(F32)
            value = value * value
            total = value[:, :128]
            for i in range(1, cb // 128):
                total = total + value[:, i * 128 : (i + 1) * 128]
            wides.append(total)
        squares = jnp.concatenate(wides, axis=0)
        broadcast_sumsq(ph, squares)

        def hop(way, r, k):
            to = (r - 1) % chips if way == 0 else (r + 1) % chips
            at = pl.ds(k * rc, rc)
            return remote(mine.at[ph, r, at], mine.at[ph, to, at], ag_sems.at[way, r, k], ag_rsem.at[ph, to, k], ring[way])

        def arrive(way, r, k):
            at = pl.ds(k * rc, rc)
            back = (r + 1) % chips if way == 0 else (r - 1) % chips
            remote(mine.at[ph, back, at], mine.at[ph, r, at], ag_sems.at[way, back, k], ag_rsem.at[ph, r, k], ring[way]).wait_recv()

        def across(r):
            return remote(mine.at[ph, r], part.at[ph, r], hp_sems.at[r], hp_rsem.at[ph, r], partner)

        for q in range(half):
            for way in (0, 1):
                start(hop(way, 0, q if way == 0 else half + q))
        for q in range(half):
            for way in (0, 1):
                start(hop(way, 0, half + q if way == 0 else q))
        start(across(0))

        def forward(d):
            for part_of in (0, 1):
                for q in range(half):
                    for way in (0, 1):
                        r = chips - d if way == 0 else d
                        far_chunk = part_of == 0
                        k = q if (way == 0) == far_chunk else half + q
                        if d == far and not far_chunk:
                            continue
                        arrive(way, r, k)
                        if d + 1 < far or (d + 1 == far and far_chunk):
                            start(hop(way, r, k))
            start(across(d))
            if d != far:
                start(across(chips - d))

        def process(j):
            r = consume[j]
            across(r).wait_recv()
            t = chip_at(r)
            s = scale_ref[...]
            s = jnp.concatenate([s] * (cb // 128), axis=1)
            xn[c] = (mine[ph, r].astype(F32) * s * gain_ref[t * 2 + c]).astype(BF16)
            xn[1 - c] = (part[ph, r].astype(F32) * s * gain_ref[t * 2 + 1 - c]).astype(BF16)
            block(j, t, jnp.concatenate([xn[0], xn[1]], axis=1))

        forward(1)
        wait_scale(ph)
        process(0)
        todo = 1
        for d in range(2, far + 1):
            process(todo)
            forward(d)
            process(todo + 1)
            todo += 2
        while todo < chips:
            process(todo)
            todo += 1

    loads[0].wait()
    loads[1].wait()
    sums = reduce_scatter(0, att[...], wo)
    loads[2].wait()
    drain()
    loads[3].wait()
    loads[4].wait()

    def mlp_block(j, t, x):
        at = pl.ds(pl.multiple_of(t * (2 * cb), 2 * cb), 2 * cb)
        g = dot_t(x, wg[:, at])
        u = dot_t(x, wu[:, at])
        if j == 0:
            gate[...] = g
            up[...] = u
        elif j < chips - 1:
            gate[...] += g
            up[...] += u
        else:
            g = gate[...] + g
            prod[...] = (g * jax.nn.sigmoid(g) * (up[...] + u)).astype(BF16)

    residual_gather(0, sums, hid, gm_ref, mlp_block)
    drain()
    loads[5].wait()
    sums = reduce_scatter(1, prod[...], wd)
    drain()

    cols = acc.shape[1]
    tiles = 2 if cols % 256 == 0 else 1
    tile = cols // tiles

    def head_block(j, t, x):
        lm_load(j).wait()
        slot = j % SLOTS

        def piece(i, carry):
            at = pl.ds(pl.multiple_of(i * tile, tile), tile)
            y = dot(x, wlm[slot, :, at])
            if j == 0:
                acc[:, at] = y
            else:
                acc[:, at] += y
            return carry

        lax.fori_loop(0, tiles, piece, 0)
        if j + SLOTS < chips:
            lm_load(j + SLOTS).start()

    residual_gather(1, sums, mine.at[0, 0], gf_ref, head_block)

    wanted = jnp.transpose(jnp.broadcast_to((ids_ref[...] - me * cols).astype(F32), (128, rows)))
    lanes[3] = wanted
    block = 64

    def stats(i, carry):
        at = pl.ds(pl.multiple_of(i * block, block), block)
        top = acc[at, 0:128]
        for j in range(1, cols // 128):
            top = jnp.maximum(top, acc[at, j * 128 : (j + 1) * 128])
        want = lanes[3, at, :] - iota((block, 128), 1).astype(F32)
        total = jnp.zeros((block, 128), F32)
        picked = jnp.zeros((block, 128), F32)
        for j in range(cols // 128):
            x = acc[at, j * 128 : (j + 1) * 128]
            total = total + jnp.exp(x - top)
            picked = picked + jnp.where(want == float(j * 128), x, 0.0)
        lanes[0, at, :] = top
        lanes[1, at, :] = total
        lanes[2, at, :] = picked
        return carry

    lax.fori_loop(0, rows // block, stats, 0)
    top = jnp.transpose(lanes[0])
    total = jnp.transpose(lanes[1])
    high = jnp.max(top, axis=0, keepdims=True)
    total = jnp.sum(total * jnp.exp(top - high), axis=0, keepdims=True)
    st_send[0:1] = high + jnp.log(total)
    st_send[1:2] = jnp.sum(jnp.transpose(lanes[2]), axis=0, keepdims=True)
    st_recv[me] = st_send[...]
    for k in range(1, n):
        start(remote(st_send, st_recv.at[me], st_sems.at[k], st_rsem.at[me], lax.rem(me + k, n)))
    for k in range(1, n):
        src = lax.rem(me + k, n)
        remote(st_send, st_recv.at[src], st_sems.at[k], st_rsem.at[src], src).wait_recv()
    every = [st_recv[j] for j in range(n)]
    high = every[0][0:1]
    for x in every[1:]:
        high = jnp.maximum(high, x[0:1])
    total = jnp.zeros_like(high)
    picked = jnp.zeros_like(high)
    for x in every:
        total = total + jnp.exp(x[0:1] - high)
        picked = picked + x[1:2]
    log_norm = high + jnp.log(total)
    ln_ref[...] = log_norm
    lp_ref[...] = picked - log_norm
    drain()


def layer_and_head(n, att, hidden, score_id, w_o, mlp_norm, w_gate, w_up, w_down, final_norm, w_lm):
    requests, nodes, width = hidden.shape
    rows = requests * nodes
    cb = width // n
    chips = n // 2
    rc = rows // CHUNKS
    ffn = w_gate.shape[1]
    cols = w_lm.shape[1]
    vmem = pl.BlockSpec(memory_space=pltpu.VMEM)
    hbm = pl.BlockSpec(memory_space=pl.ANY)
    dma = pltpu.SemaphoreType.DMA
    row = jax.ShapeDtypeStruct((1, rows), F32)
    log_norm, log_prob = pl.pallas_call(
        functools.partial(layer_kernel, n),
        name="layer_and_head",
        out_shape=(row, row),
        in_specs=[vmem] * 3 + [hbm] * 7,
        out_specs=(vmem, vmem),
        scratch_shapes=[
            pltpu.VMEM(att.shape, BF16),
            pltpu.VMEM((rows, cb), BF16),
            pltpu.VMEM(w_o.shape, BF16),
            pltpu.VMEM((ffn, width), BF16),
            pltpu.VMEM((ffn, width), BF16),
            pltpu.VMEM((ffn, width), BF16),
            pltpu.VMEM((SLOTS, 2 * cb, cols), BF16),
            pltpu.VMEM((rows, cols), F32),
            pltpu.VMEM((rows, ffn), F32),
            pltpu.VMEM((rows, ffn), F32),
            pltpu.VMEM((rows, ffn), BF16),
            pltpu.VMEM((2, rows, cb), BF16),
            pltpu.VMEM((rows, 128), F32),
            pltpu.VMEM((chips, rows, cb), F32),
            pltpu.VMEM((chips, rows, cb), BF16),
            pltpu.VMEM((2, chips, rows, cb), BF16),
            pltpu.VMEM((2, chips // 2, CHUNKS, rc, cb), BF16),
            pltpu.VMEM((2, 2, chips // 2, CHUNKS, rc, cb), BF16),
            pltpu.VMEM((2, chips, rows, cb), BF16),
            pltpu.VMEM((2, chips, rows, cb), BF16),
            pltpu.VMEM((1, rows), F32),
            pltpu.VMEM((2, n, 1, rows), F32),
            pltpu.VMEM((2, rows), F32),
            pltpu.VMEM((n, 2, rows), F32),
            pltpu.VMEM((4, rows, 128), F32),
            dma((6,)),
            dma((SLOTS,)),
            dma((chips,)),
            dma((2, chips)),
            dma((2, chips // 2, CHUNKS)),
            dma((2, 2, chips // 2, CHUNKS)),
            dma((2, chips, CHUNKS)),
            dma((2, chips, CHUNKS)),
            dma((chips,)),
            dma((2, chips)),
            dma((n,)),
            dma((2, n)),
            dma((n,)),
            dma((n,)),
        ],
        compiler_params=pltpu.CompilerParams(collective_id=0, has_side_effects=True, vmem_limit_bytes=67043328),
    )(
        score_id.reshape(1, rows),
        mlp_norm.astype(F32).reshape(n, 1, cb),
        final_norm.astype(F32).reshape(n, 1, cb),
        att,
        hidden.reshape(rows, width),
        w_o,
        w_gate.T,
        w_up.T,
        w_down,
        w_lm,
    )
    return log_norm.reshape(requests, nodes), log_prob.reshape(requests, nodes)


def solution(mesh):
    n = mesh.shape["tp"]

    def group_step(hidden, tree_mask, depth, ctx_len, block_table, score_id, k_cache, v_cache, attn_norm, w_q, w_k, w_v, w_o, mlp_norm, w_gate, w_up, w_down, final_norm, w_lm):
        att, k_out, v_out = attention(hidden, tree_mask, ctx_len, block_table, k_cache, v_cache, attn_norm, w_q, w_k, w_v)
        log_norm, log_prob = layer_and_head(n, att, hidden, score_id, w_o, mlp_norm, w_gate, w_up, w_down, final_norm, w_lm)
        return log_norm, log_prob, k_out, v_out

    request_spec = P("dp", None, None)
    node_spec = P("dp", None)
    cache_spec = P("dp", None, "tp", None)
    shared_spec = P(None)
    column_spec = P(None, "tp")
    row_spec = P("tp", None)
    in_specs = (request_spec, request_spec, node_spec, P("dp"), node_spec, node_spec, cache_spec, cache_spec, shared_spec, column_spec, column_spec, column_spec, row_spec, shared_spec, column_spec, column_spec, row_spec, shared_spec, column_spec)
    out_specs = (node_spec, node_spec, cache_spec, cache_spec)
    return jax.shard_map(group_step, mesh=mesh, in_specs=in_specs, out_specs=out_specs, check_vma=False)
```

time: 375 us -> 116 us (0.31)
  waiting for transfers between devices: 180 us -> 0 us
  Pallas kernels: 0 us -> 105 us
  local copies, waits for them, and re-layouts: 64.2 us -> 3.18 us
  blocking collectives: 50.7 us -> 0 us
  matrix products: 49.1 us -> 0 us
  between operations: 14.5 us -> 0.65 us
  other arithmetic: 14.6 us -> 6.5 us
    psum x2 -> x0, waiting for transfers between devices: 180 us -> none  [the longest x1 113 us: layer_and_logits(): lax.psum(jnp.dot(attended, w_o, preferred_element_type=jnp.float32).astyp...]
    pallas_call x0 -> x2, Pallas kernels: none -> 105 us  [the longest x1 95.2 us: layer_and_head(): pl.pallas_call(functools.partial(layer_kernel, n), name='layer_and_head',...]
    dot_general x12 -> x0, matrix products: 49.1 us -> none  [the longest x1 25.8 us: layer_and_logits(): jnp.dot(rms_norm(layer_out, final_norm), w_lm, preferred_element_type=jnp...]
    scatter x2 -> x0, local copies, waits for them, and re-layouts: 39.9 us -> none  [write_cache(): return cache.at[slot_blocks, slots % page_size].set(new_rows)]
    psum x1 -> x0, blocking collectives: 26.9 us -> none  [group_step(): lax.psum(jnp.stack([part_sum, jnp.where(inside, picked, 0.0)]), 'tp')]
    pmax x1 -> x0, blocking collectives: 23.9 us -> none  [group_step(): global_top = lax.pmax(jnp.max(logits, axis=-1), 'tp')]
    gather x8 -> x0, local copies, waits for them, and re-layouts: 14.6 us -> none  [the longest x1 4.8 us: layer_and_logits(): val_old = v_cache[block_table].reshape(requests, span, kv_local, head_dim)]
    reduce_sum x6 -> x0, other arithmetic: 12.8 us -> none  [the longest x3 8.54 us: rms_norm(): jnp.mean(widened * widened, axis=-1, keepdims=True) + RMS_EPS]
  transfers between devices with their start and end apart: 2 -> 0, of which waited for: 2 -> 0; matrix products, arithmetic and copies ran while one was open for 11% -> 0% of each run, Pallas kernels for 0% -> 0%
where the time goes in v1:
time: 116 us; the launch traced here: 115 us
  Pallas kernels  105 us (91%)
  other arithmetic  6.5 us (6%)
  local copies, waits for them, and re-layouts  3.18 us (3%)
    pallas_call x1, Pallas kernels, layer_and_head(): pl.pallas_call(functools.partial(layer_kernel, n), name='layer_and_head',...  95.2 us
    pallas_call x1, Pallas kernels, attention(): pl.pallas_call(functools.partial(attention_kernel, (requests, nodes, page...  9.91 us
    pallas_call x2, other arithmetic, layer_and_head(): pl.pallas_call(functools.partial(layer_kernel, n), name='layer_and_head',...  2.61 us

profile of v1, /device:TPU:21, one launch (start us, length us, event | category | flops | bytes accessed | tf_op | source)
XLA Modules:
  0.0 115.4 jit_solution(10007619342186189517)
XLA Ops:
  0.6 1.3 %broadcast_in_dim.7 = f32[4096]{0:T(1024)} convert(bf16[4096]{0:T(1024)(128)(2,1)} %param.27) | non-fusion elementwise | flops 4096 | bytes 24576 | tf_op jit(solution)/shard_map/broadcast_in_dim | solution.py:190
  1.9 9.9 %tree_attention.1 = (bf16[256,256]{1,0:T(8,128)(2,1)}, bf16[128,32,128]{2,1,0:T(8,128)(2,1)}, bf16[128,32,128]{2,1,0:T(8,128)(2,1)}) custom-call(s32[8]{0:T(128)} %ctx_ref.1, s32[8,16]{1,0:T(8,128)} %table_ref.1, s32[256,32]{1,0:T(8,128)} %bitcast.17, f32[1,128]{1,0:T(1,128)} %constant.2.clone.freq_ref, f32[1,4096]{1,0:T(1,128)} %bitcast.20, ...), custom_call_target="tpu_custom_call" | custom-call | tf_op jit(solution)/shard_map/tree_attention/pallas_call | solution.py:166
  11.8 1.3 %reshape.59 = f32[4096]{0:T(1024)} convert(bf16[4096]{0:T(1024)(128)(2,1)} %param.32) | non-fusion elementwise | flops 4096 | bytes 24576 | tf_op jit(solution)/shard_map/reshape | solution.py:592
  13.1 1.3 %reshape.61 = f32[4096]{0:T(1024)} convert(bf16[4096]{0:T(1024)(128)(2,1)} %param.36) | non-fusion elementwise | flops 4096 | bytes 24576 | tf_op jit(solution)/shard_map/reshape | solution.py:593
  14.4 1.3 %reshape.46.ids_ref = s32[1,256]{1,0:T(1,128)} reshape(s32[8,32]{1,0:T(8,128)} %param.24) | data formatting | bytes 2048 | tf_op jit(solution)/shard_map/reshape | solution.py:591
  15.8 95.2 %layer_and_head.1 = (f32[1,256]{1,0:T(1,128)}, f32[1,256]{1,0:T(1,128)}) custom-call(s32[1,256]{1,0:T(1,128)} %reshape.46.ids_ref, f32[16,1,256]{2,1,0:T(1,128)} %bitcast.18, f32[16,1,256]{2,1,0:T(1,128)} %bitcast.19, bf16[256,256]{1,0:T(8,128)(2,1)} %get-tuple-element.9.att_hbm, bf16[256,4096]{1,0:T(8,128)(2,1)} %bitcast.12, bf16[256,4096]{1,0:T(8,128)(2,1)} %wo_hbm.1, ...), custom_call_target="tpu_custom_call" | custom-call | tf_op jit(solution)/shard_map/layer_and_head/pallas_call | solution.py:542
  111.0 0.5 broadcast.6
  111.5 1.3 %reduce.6 = f32[256]{0:T(256)S(1)} reduce(f32[1,256]{1,0:T(1,128)} %get-tuple-element.10, f32[]{:T(128)} %broadcast.6), dimensions={0}, to_apply=%get-tuple-element.10.reduce_sub_computation.3 | reduce | bytes 2052 | tf_op jit(solution)/shard_map/layer_and_head/pallas_call | solution.py:542
  112.8 0.7 reshape.55
  113.5 1.3 %reduce.7 = f32[256]{0:T(256)S(1)} reduce(f32[1,256]{1,0:T(1,128)} %get-tuple-element.11, f32[]{:T(128)} %broadcast.6), dimensions={0}, to_apply=%get-tuple-element.11.reduce_sub_computation.3 | reduce | bytes 2052 | tf_op jit(solution)/shard_map/layer_and_head/pallas_call | solution.py:542
  114.8 0.7 reshape.56
